TPU v7x, 256 devices: a whole 4x4x8 slice. The times are simulated.
256 devices in a mesh: vocab: 32 (over z, y), section: 8 (over x, core).
Axes of the slice: x: 4, y: 4, z: 8, core: 2. Of those that a mesh axis runs over, the one named last changes fastest.
Arguments:
- hidden: bfloat16 [512, 8192], P('section', 'vocab'), may hold values from -2 to 2
- targets: int32 [512], replicated, may hold values from 0 to 98303
- out_weight: bfloat16 [98304, 8192], P(('vocab', 'section')), may hold values from -2 to 2
Outputs:
- token_loss: float32 [512], replicated
- weight_grad: bfloat16 [98304, 8192], P(('vocab', 'section'))
- sent_grad: bfloat16 [512, 8192], P('section', 'vocab')
All inputs are finite; a program needn't handle non-finite values.
Results may differ from a plain program's by a relative error of at most 0.0033.
Values may be sent and summed in bfloat16 or wider, within the bound.
A program may use at most 128 MiB of HBM per device.

v0:
```python
import jax
import jax.numpy as jnp
from jax import lax
from jax.sharding import Mesh
from jax.sharding import PartitionSpec as P

VOCAB = ("vocab_0", "vocab_1")
SECTION = ("section_0", "section_1")
VOCAB_SECTION = ("vocab_0", "vocab_1", "section_0", "section_1")


def sent_to_all(value, axis):
    copies = jnp.broadcast_to(value, (lax.axis_size(axis), *value.shape))
    return lax.all_to_all(copies, axis, split_axis=0, concat_axis=0, tiled=True)


def laid_out(blocks, dim):
    blocks = jnp.moveaxis(blocks, 0, dim)
    dims = blocks.shape
    return blocks.reshape(*dims[:dim], dims[dim] * dims[dim + 1], *dims[dim + 2 :])


def gathered_copies(value, axis, dim):
    blocks = sent_to_all(value, axis)
    return laid_out(blocks, dim)


def collected_together(value, axis):
    leaves = jax.tree.leaves(value)
    sequence = sorted(range(len(leaves)), key=lambda k: -leaves[k].size)
    width = (1, *leaves[sequence[0]].shape)[-1]
    lines = [
        jnp.pad(leaves[k].reshape(-1), (0, -leaves[k].size % width)).reshape(-1, width)
        for k in sequence
    ]
    both, at, found = (lax.all_gather(jnp.concatenate(lines), axis), 0, {})
    for k, line in zip(sequence, lines):
        piece = both[:, at : at + len(line)].reshape(len(both), -1)
        found[k] = piece[:, : leaves[k].size].reshape(-1, *leaves[k].shape)
        at += len(line)
    numbers = iter(range(len(leaves)))
    return jax.tree.map(lambda _: found[next(numbers)], value)


def combined_by_axis(value, axes, combine):
    for axis in axes:
        pieces = collected_together(value, axis)
        value = jax.tree.map(lambda part: part[0], pieces)
        for k in range(1, lax.axis_size(axis)):
            value = combine(value, jax.tree.map(lambda part: part[k], pieces))
    return value


def split_up(value, dim, devices):
    before, after = (value.shape[:dim], value.shape[dim + 1 :])
    return jnp.moveaxis(value.reshape(*before, devices, -1, *after), dim, 0)


def summed_on_arrival(value, axis, dim):
    blocks = split_up(value, dim, lax.axis_size(axis))
    arrived = lax.all_to_all(blocks, axis, split_axis=0, concat_axis=0, tiled=True)
    return arrived.sum(axis=0)


def shifted(value, axis, steps):
    count = lax.axis_size(axis)
    pairs = [(source, (source + steps) % count) for source in range(count)]
    return lax.ppermute(value, axis, pairs)


def combine(first, second):
    top_a, sum_a, hit_a = first
    top_b, sum_b, hit_b = second
    top = jnp.maximum(top_a, top_b)
    return (top, sum_a * jnp.exp(top_a - top) + sum_b * jnp.exp(top_b - top), hit_a + hit_b)


def on_device(hidden, targets, out_weight):
    columns = gathered_copies(hidden, VOCAB, 1)
    whole = lax.all_gather(columns, SECTION, axis=0, tiled=True)
    rows = out_weight.shape[0]
    offset = lax.axis_index(VOCAB_SECTION) * rows
    logits = jnp.einsum("td,vd->tv", whole, out_weight, preferred_element_type=jnp.float32)
    picked = targets[:, None] - offset == jnp.arange(rows, dtype=jnp.int32)[None, :]
    local_hit = jnp.sum(jnp.where(picked, logits, jnp.float32(0.0)), axis=1)
    local_top = jnp.max(logits, axis=1)
    local_sum = jnp.sum(jnp.exp(logits - local_top[:, None]), axis=1)
    top, total, target_logit = combined_by_axis(
        (local_top, local_sum, local_hit), VOCAB_SECTION, combine
    )
    token_loss = top + jnp.log(total) - target_logit
    probs = jnp.exp(logits - top[:, None]) / total[:, None]
    dlogits = (probs - picked.astype(jnp.float32)).astype(jnp.bfloat16)
    weight_grad = jnp.einsum(
        "tv,td->vd", dlogits, whole, preferred_element_type=jnp.float32
    ).astype(jnp.bfloat16)
    token_block = lax.psum_scatter(
        jnp.dot(dlogits, out_weight, preferred_element_type=jnp.float32),
        SECTION,
        scatter_dimension=0,
        tiled=True,
    )
    owned = summed_on_arrival(token_block, VOCAB, 1)
    sent_grad = shifted(owned.astype(jnp.bfloat16), SECTION, -1)
    return (token_loss, weight_grad, sent_grad)


def solution(mesh):
    split = Mesh(mesh.devices.reshape(8, 4, 4, 2), ("vocab_0", "vocab_1", "section_0", "section_1"))
    placed = (P(SECTION, VOCAB), P(), P(VOCAB_SECTION, None))
    return jax.shard_map(
        on_device,
        mesh=split,
        in_specs=placed,
        out_specs=(P(), P(VOCAB_SECTION, None), P(SECTION, VOCAB)),
        check_vma=False,
    )
```

profile of v0, /device:TPU:1, one launch (start us, length us, event | category | flops | bytes accessed | tf_op | source)
XLA Modules:
  0.0 341.3 jit_solution(13021333229469894591)
XLA Ops:
  7.2 0.0 copy-start
  7.2 0.0 all-gather.10.cloned.1.call-start
  7.2 0.9 broadcast_in_dim.6
  8.1 38.0 %all_to_all.10 = bf16[32,64,256]{2,1,0:T(8,128)(2,1)S(1)} all-to-all(bf16[32,64,256]{2,1,0:T(8,128)(2,1)S(1)} %broadcast_in_dim.6), channel_id=1, replica_groups=mesh['vocab_0'=8,'vocab_1'=4,'section_0'=4,'section_1'=2] {'vocab_0','vo..., dimensions={0} | all-to-all | bytes 2097152 | tf_op jit(solution)/shard_map/all_to_all | solution.py:14
  46.1 1.0 copy.9
  47.2 0.0 all-gather.10.cloned.1.call-update
  47.2 0.0 reduce-scatter.2.cloned.1.call-start
  47.2 0.0 copy-done
  47.3 51.9 %all-gather.10.cloned.1.call-done = bf16[512,8192]{1,0:T(8,128)(2,1)} async-done(((bf16[64,8192]{1,0:T(8,128)(2,1)}), bf16[512,8192]{1,0:T(8,128)(2,1)}) %all-gather.10.cloned.1.call-update) | async-done | bytes 8388624 | tf_op jit(solution)/shard_map/all_gather | solution.py:80
  99.1 7.8 %fusion.60 = (f32[512]{0:T(512)S(1)}, f32[512,384]{0,1:T(8,128)S(1)}) fusion(bf16[512,8192]{1,0:T(8,128)(2,1)} %all-gather.10.cloned.1.call-done, bf16[384,8192]{1,0:T(8,128)(2,1)} %param.5), kind=kOutput, calls=%fused_computation.116 | convolution fusion | flops 3221421568 | bytes 15468544 | tf_op jit(solution)/shard_map/td,vd->tv/dot_general | solution.py:83
  107.0 0.2 exponential_reduce_fusion
  107.2 19.7 %all-gather.4 = f32[8,3,512]{2,1,0:T(4,128)S(1)} all-gather(f32[1,3,512]{2,1,0:T(4,128)S(1)} %maximum_bitcast_fusion), channel_id=2, replica_groups=mesh['vocab_0'=8,'vocab_1'=4,'section_0'=4,'section_1'=2] {'vocab_0'}, dimensions={0}, use_global_device_ids=true | all-gather | bytes 55296 | tf_op jit(solution)/shard_map/all_gather | solution.py:36
  126.9 0.1 fusion.22
  127.0 9.6 %all-gather.5 = f32[4,3,512]{2,1,0:T(4,128)S(1)} all-gather(f32[1,3,512]{2,1,0:T(4,128)S(1)} %maximum_bitcast_fusion.1), channel_id=3, replica_groups=mesh['vocab_0'=8,'vocab_1'=4,'section_0'=4,'section_1'=2] {'vocab_1'}, dimensions={0}, use_global_device_ids=true | all-gather | bytes 30720 | tf_op jit(solution)/shard_map/all_gather | solution.py:36
  136.7 9.0 %all-gather.6 = f32[4,3,512]{2,1,0:T(4,128)S(1)} all-gather(f32[1,3,512]{2,1,0:T(4,128)S(1)} %maximum_bitcast_fusion.2), channel_id=4, replica_groups=mesh['vocab_0'=8,'vocab_1'=4,'section_0'=4,'section_1'=2] {'section_0'}, dimensions={0}, use_global_device_ids=true | all-gather | bytes 30720 | tf_op jit(solution)/shard_map/all_gather | solution.py:36
  145.8 13.6 %all-gather.7 = f32[2,3,512]{2,1,0:T(4,128)S(1)} all-gather(f32[1,3,512]{2,1,0:T(4,128)S(1)} %maximum_bitcast_fusion.3), channel_id=5, replica_groups=mesh['vocab_0'=8,'vocab_1'=4,'section_0'=4,'section_1'=2] {'section_1'}, dimensions={0}, use_global_device_ids=true | all-gather | bytes 18432 | tf_op jit(solution)/shard_map/all_gather | solution.py:36
  159.4 0.6 add_subtract_fusion
  160.0 10.9 %fusion.55 = f32[512,8192]{1,0:T(8,128)} fusion(bf16[384,8192]{1,0:T(8,128)(2,1)} %param.5, f32[512,384]{0,1:T(8,128)S(1)} %get-tuple-element.20, f32[512]{0:T(512)S(1)} %get-tuple-element.6, f32[512]{0:T(512)S(1)} %get-tuple-element.7, s32[512]{0:T(512)S(1)} %broadcast_subtract_fusion), kind=kOutput, calls=%fused_computation.114 | convolution fusion | flops 3222405120 | bytes 23861248 | tf_op jit(solution)/shard_map/dot_general | solution.py:98
  170.9 0.0 reduce-scatter.2.cloned.1.call-update
  171.0 91.3 %reduce-scatter.2.cloned.1.call-done = f32[64,8192]{1,0:T(8,128)} async-done(((f32[512,8192]{1,0:T(8,128)}), f32[64,8192]{1,0:T(8,128)}) %reduce-scatter.2.cloned.1.call-update) | async-done | bytes 2097168 | tf_op jit(solution)/shard_map/reduce_scatter | solution.py:97
  262.3 1.8 copy.11
  264.1 57.7 %all_to_all.11 = f32[32,64,256]{2,1,0:T(8,128)S(1)} all-to-all(f32[32,64,256]{2,1,0:T(8,128)S(1)} %bitcast.336), channel_id=1, replica_groups=mesh['vocab_0'=8,'vocab_1'=4,'section_0'=4,'section_1'=2] {'vocab_0','vo..., dimensions={0} | all-to-all | bytes 4194304 | tf_op jit(solution)/shard_map/all_to_all | solution.py:61
  321.8 0.1 reduce_sum.29
  322.0 3.1 collective-permute-start
  325.1 8.7 %convolution_convert_fusion = bf16[384,8192]{1,0:T(8,128)(2,1)} fusion(bf16[512,8192]{1,0:T(8,128)(2,1)} %all-gather.10.cloned.1.call-done, f32[512,384]{0,1:T(8,128)S(1)} %get-tuple-element.20, f32[512]{0:T(512)S(1)} %get-tuple-element.6, f32[512]{0:T(512)S(1)} %get-tuple-element.7, s32[512]{0:T(512)S(1)} %broadcast_subtract_fusion), kind=kOutput, calls=%fused_computation | convolution fusion | flops 3225550848 | bytes 15472640 | tf_op jit(solution)/shard_map/tv,td->vd/dot_general | solution.py:94
  333.8 0.0 collective-permute-done
  333.8 0.6 copy.13
  (11 shorter events, 0.2 us)
Async XLA Ops:
  7.2 40.1 %copy-start = (s32[512]{0:T(512)S(1)}, s32[512]{0:T(512)}, u32[]{:S(2)}) copy-start(s32[512]{0:T(512)} %param.4) | copy-start | bytes 6148
  7.2 91.9 %all-gather.10.cloned.1.call-start = ((), (), s32[]{:S(2)}) async-start(), calls=%async_computation.3 | async-start | bytes 9437184 | tf_op jit(solution)/shard_map/all_gather | solution.py:80
  47.2 215.1 %reduce-scatter.2.cloned.1.call-start = ((), (), s32[]{:S(2)}) async-start(), calls=%async_computation.4 | async-start | bytes 18874368 | tf_op jit(solution)/shard_map/reduce_scatter | solution.py:97
  322.0 11.9 %collective-permute-start = (bf16[64,256]{1,0:T(8,128)(2,1)S(1)}, bf16[64,256]{1,0:T(8,128)(2,1)S(1)}, u32[]{:S(2)}, u32[]{:S(2)}) collective-permute-start(bf16[64,256]{1,0:T(8,128)(2,1)S(1)} %reduce_sum.29), channel_id=1, source_target_pairs={{0,7},{1,0},{2,1},{3,2},{4,3},{5,4},{6,5},{7,6},{8,15},{9,8},{10,9... | collective-permute-start | bytes 98312 | tf_op jit(solution)/shard_map/ppermute | solution.py:68
Sparse Core Ops, SparseCore 0:
  47.3 51.7 all-gather.9
  171.1 91.1 reduce-scatter.1
where the time goes:
time: 342 us; the launch traced here: 341 us
  blocking collectives  148 us (43%)
  waiting for transfers between devices  143 us (42%)
  matrix products  27.5 us (8%)
  between operations  14.2 us (4%)
  local copies, waits for them, and re-layouts  4.34 us (1%)
    reduce_scatter x1, waiting for transfers between devices, on_device(): lax.psum_scatter(jnp.dot(dlogits, out_weight, preferred_element_type=jnp....  91.3 us
    all_to_all x1, blocking collectives, summed_on_arrival(): lax.all_to_all(blocks, axis, split_axis=0, concat_axis=0, tiled=True)  57.7 us
    all_gather x4, blocking collectives, collected_together(): both, at, found = (lax.all_gather(jnp.concatenate(lines), axis), 0, {})  52 us
    all_gather x1, waiting for transfers between devices, on_device(): whole = lax.all_gather(columns, SECTION, axis=0, tiled=True)  51.9 us
    all_to_all x1, blocking collectives, sent_to_all(): return lax.all_to_all(copies, axis, split_axis=0, concat_axis=0, tiled=True)  38 us
    dot_general x1, matrix products, on_device(): jnp.dot(dlogits, out_weight, preferred_element_type=jnp.float32)  10.9 us
    dot_general x1, matrix products, on_device(): jnp.einsum('tv,td->vd', dlogits, whole, preferred_element_type=jnp.float32)  8.73 us
    dot_general x1, matrix products, on_device(): jnp.einsum('td,vd->tv', whole, out_weight, preferred_element_type=jnp.flo...  7.84 us
  transfers between devices with their start and end apart: 3, of which 2 were waited for; matrix products, arithmetic and copies ran while one was open for 3% of the time, Pallas kernels for 0%

commit v1 on v0

--- a/solution.py
+++ b/solution.py
@@ -77,7 +77,9 @@
 
 def on_device(hidden, targets, out_weight):
     columns = gathered_copies(hidden, VOCAB, 1)
-    whole = lax.all_gather(columns, SECTION, axis=0, tiled=True)
+    whole = jnp.concatenate(
+        lax.all_to_all(jnp.stack([columns] * lax.axis_size(SECTION)), SECTION, 0, 0), axis=0
+    )
     rows = out_weight.shape[0]
     offset = lax.axis_index(VOCAB_SECTION) * rows
     logits = jnp.einsum("td,vd->tv", whole, out_weight, preferred_element_type=jnp.float32)

time: 342 us -> 390 us (1.14)
  waiting for transfers between devices: 143 us -> 183 us
  starting transfers between devices: 3.2 us -> 10.9 us
    all_to_all x0 -> x1, waiting for transfers between devices: none -> 93.7 us  [on_device(): lax.all_to_all(jnp.stack([columns] * lax.axis_size(SECTION)), SECTION, 0, 0)]
    all_gather x1 -> x0, waiting for transfers between devices: 51.9 us -> none  [on_device(): whole = lax.all_gather(columns, SECTION, axis=0, tiled=True)]
    all_to_all x0 -> x1, starting transfers between devices: none -> 7.76 us  [on_device(): lax.all_to_all(jnp.stack([columns] * lax.axis_size(SECTION)), SECTION, 0, 0)]
    another operation x0 -> x2, local copies, waits for them, and re-layouts: none -> 4.3 us  [on_device(): jnp.stack([columns] * lax.axis_size(SECTION))]
  transfers between devices with their start and end apart: 3 -> 3, of which waited for: 2 -> 2; matrix products, arithmetic and copies ran while one was open for 3% -> 2% of each run, Pallas kernels for 0% -> 0%
where the time goes in v1:
time: 390 us
  waiting for transfers between devices  183 us (47%)
  blocking collectives  147 us (38%)
  matrix products  25.6 us (7%)
  between operations  14.1 us (4%)
  starting transfers between devices  10.9 us (3%)
  local copies, waits for them, and re-layouts  7.61 us (2%)
    all_to_all x1, waiting for transfers between devices, on_device(): lax.all_to_all(jnp.stack([columns] * lax.axis_size(SECTION)), SECTION, 0, 0)  93.7 us
    reduce_scatter x1, waiting for transfers between devices, on_device(): lax.psum_scatter(jnp.dot(dlogits, out_weight, preferred_element_type=jnp....  89.2 us
    all_to_all x1, blocking collectives, summed_on_arrival(): lax.all_to_all(blocks, axis, split_axis=0, concat_axis=0, tiled=True)  57.7 us
    all_gather x4, blocking collectives, collected_together(): both, at, found = (lax.all_gather(jnp.concatenate(lines), axis), 0, {})  51.5 us
    all_to_all x1, blocking collectives, sent_to_all(): return lax.all_to_all(copies, axis, split_axis=0, concat_axis=0, tiled=True)  38 us
    dot_general x1, matrix products, on_device(): jnp.einsum('td,vd->tv', whole, out_weight, preferred_element_type=jnp.flo...  8.75 us
    dot_general x1, matrix products, on_device(): jnp.einsum('tv,td->vd', dlogits, whole, preferred_element_type=jnp.float32)  8.71 us
    dot_general x1, matrix products, on_device(): jnp.dot(dlogits, out_weight, preferred_element_type=jnp.float32)  8.16 us
  transfers between devices with their start and end apart: 3, of which 2 were waited for; matrix products, arithmetic and copies ran while one was open for 2% of the time, Pallas kernels for 0%

profile of v1, /device:TPU:1, one launch (start us, length us, event | category | flops | bytes accessed | tf_op | source)
XLA Modules:
  0.0 389.6 jit_solution(1125466257712527983)
XLA Ops:
  7.2 0.9 broadcast_in_dim.6
  8.0 38.0 %all_to_all.15 = bf16[32,64,256]{2,1,0:T(8,128)(2,1)S(1)} all-to-all(bf16[32,64,256]{2,1,0:T(8,128)(2,1)S(1)} %broadcast_in_dim.6), channel_id=1, replica_groups=mesh['vocab_0'=8,'vocab_1'=4,'section_0'=4,'section_1'=2] {'vocab_0','vo..., dimensions={0} | all-to-all | bytes 2097152 | tf_op jit(solution)/shard_map/all_to_all | solution.py:14
  46.1 0.1 copy.9
  46.1 4.2 %stack.3 = bf16[8,64,8192]{2,1,0:T(8,128)(2,1)} broadcast(bf16[64,8192]{1,0:T(8,128)(2,1)S(1)} %bitcast.340), dimensions={1,2} | broadcast | bytes 9437184 | tf_op jit(solution)/shard_map/stack | solution.py:81
  50.4 0.0 copy-start
  50.4 0.0 slice-start
  50.4 7.8 %all-to-all-start.1 = ((bf16[8,64,8192]{2,1,0:T(8,128)(2,1)}), bf16[8,64,8192]{2,1,0:T(8,128)(2,1)}, u32[]{:S(2)}, u32[]{:S(2)}) async-start(bf16[8,64,8192]{2,1,0:T(8,128)(2,1)} %stack.3), calls=%async_computation.1 | async-start | bytes 16777216 | tf_op jit(solution)/shard_map/all_to_all | solution.py:81
  58.1 0.0 reduce-scatter.2.cloned.1.call-start
  58.1 0.0 copy-done
  58.1 93.7 %all-to-all-done.1 = bf16[8,64,8192]{2,1,0:T(8,128)(2,1)} async-done(((bf16[8,64,8192]{2,1,0:T(8,128)(2,1)}), bf16[8,64,8192]{2,1,0:T(8,128)(2,1)}, u32[]{:S(2)}, u32[]{:S(2)}) %all-to-all-start.1) | async-done | bytes 8388640 | tf_op jit(solution)/shard_map/all_to_all | solution.py:81
  151.9 0.0 slice-start.1
  151.9 8.7 %fusion.60 = (f32[512]{0:T(512)S(1)}, f32[512,384]{0,1:T(8,128)S(1)}) fusion(bf16[512,8192]{1,0:T(8,128)(2,1)} %bitcast.1, bf16[384,8192]{1,0:T(8,128)(2,1)} %param.5), kind=kOutput, calls=%fused_computation.116 | convolution fusion | flops 3221421568 | bytes 15468544 | tf_op jit(solution)/shard_map/td,vd->tv/dot_general | solution.py:85
  160.6 0.2 exponential_reduce_fusion
  160.9 18.9 %all-gather.4 = f32[8,3,512]{2,1,0:T(4,128)S(1)} all-gather(f32[1,3,512]{2,1,0:T(4,128)S(1)} %maximum_bitcast_fusion), channel_id=2, replica_groups=mesh['vocab_0'=8,'vocab_1'=4,'section_0'=4,'section_1'=2] {'vocab_0'}, dimensions={0}, use_global_device_ids=true | all-gather | bytes 55296 | tf_op jit(solution)/shard_map/all_gather | solution.py:36
  179.8 0.1 fusion.22
  179.9 9.7 %all-gather.5 = f32[4,3,512]{2,1,0:T(4,128)S(1)} all-gather(f32[1,3,512]{2,1,0:T(4,128)S(1)} %maximum_bitcast_fusion.1), channel_id=3, replica_groups=mesh['vocab_0'=8,'vocab_1'=4,'section_0'=4,'section_1'=2] {'vocab_1'}, dimensions={0}, use_global_device_ids=true | all-gather | bytes 30720 | tf_op jit(solution)/shard_map/all_gather | solution.py:36
  189.7 9.0 %all-gather.6 = f32[4,3,512]{2,1,0:T(4,128)S(1)} all-gather(f32[1,3,512]{2,1,0:T(4,128)S(1)} %maximum_bitcast_fusion.2), channel_id=4, replica_groups=mesh['vocab_0'=8,'vocab_1'=4,'section_0'=4,'section_1'=2] {'section_0'}, dimensions={0}, use_global_device_ids=true | all-gather | bytes 30720 | tf_op jit(solution)/shard_map/all_gather | solution.py:36
  198.8 13.8 %all-gather.7 = f32[2,3,512]{2,1,0:T(4,128)S(1)} all-gather(f32[1,3,512]{2,1,0:T(4,128)S(1)} %maximum_bitcast_fusion.3), channel_id=5, replica_groups=mesh['vocab_0'=8,'vocab_1'=4,'section_0'=4,'section_1'=2] {'section_1'}, dimensions={0}, use_global_device_ids=true | all-gather | bytes 18432 | tf_op jit(solution)/shard_map/all_gather | solution.py:36
  212.7 0.6 add_subtract_fusion
  213.3 0.0 slice-done
  213.3 0.0 slice-done.1
  213.3 8.2 %fusion.55 = f32[512,8192]{1,0:T(8,128)} fusion(bf16[384,8192]{1,0:T(8,128)(2,1)S(1)} %bitcast.339, f32[512,384]{0,1:T(8,128)S(1)} %get-tuple-element.20, f32[512]{0:T(512)S(1)} %get-tuple-element.6, f32[512]{0:T(512)S(1)} %get-tuple-element.7, s32[512]{0:T(512)S(1)} %broadcast_subtract_fusion), kind=kOutput, calls=%fused_computation.114 | convolution fusion | flops 3222405120 | bytes 23861248 | tf_op jit(solution)/shard_map/dot_general | solution.py:100
  221.4 0.0 reduce-scatter.2.cloned.1.call-update
  221.5 89.2 %reduce-scatter.2.cloned.1.call-done = f32[64,8192]{1,0:T(8,128)} async-done(((f32[512,8192]{1,0:T(8,128)}), f32[64,8192]{1,0:T(8,128)}) %reduce-scatter.2.cloned.1.call-update) | async-done | bytes 2097168 | tf_op jit(solution)/shard_map/reduce_scatter | solution.py:99
  310.6 1.8 copy.11
  312.4 57.7 %all_to_all.16 = f32[32,64,256]{2,1,0:T(8,128)S(1)} all-to-all(f32[32,64,256]{2,1,0:T(8,128)S(1)} %bitcast.337), channel_id=1, replica_groups=mesh['vocab_0'=8,'vocab_1'=4,'section_0'=4,'section_1'=2] {'vocab_0','vo..., dimensions={0} | all-to-all | bytes 4194304 | tf_op jit(solution)/shard_map/all_to_all | solution.py:61
  370.1 0.1 reduce_sum.29
  370.3 3.1 collective-permute-start
  373.4 8.7 %convolution_convert_fusion = bf16[384,8192]{1,0:T(8,128)(2,1)} fusion(bf16[512,8192]{1,0:T(8,128)(2,1)} %bitcast.1, f32[512,384]{0,1:T(8,128)S(1)} %get-tuple-element.20, f32[512]{0:T(512)S(1)} %get-tuple-element.6, f32[512]{0:T(512)S(1)} %get-tuple-element.7, s32[512]{0:T(512)S(1)} %broadcast_subtract_fusion), kind=kOutput, calls=%fused_computation | convolution fusion | flops 3225550848 | bytes 15472640 | tf_op jit(solution)/shard_map/tv,td->vd/dot_general | solution.py:96
  382.1 0.0 collective-permute-done
  382.1 0.6 copy.13
  (12 shorter events, 0.2 us)
Async XLA Ops:
  50.4 7.8 %copy-start = (s32[512]{0:T(512)S(1)}, s32[512]{0:T(512)}, u32[]{:S(2)}) copy-start(s32[512]{0:T(512)} %param.4) | copy-start | bytes 6148
  50.4 162.9 %slice-start = ((s8[6291456]{0:T(1024)(128)(4,1)}), s8[2097152]{0:T(1024)(128)(4,1)S(1)}, s32[]{:S(2)}) async-start(s8[6291456]{0:T(1024)(128)(4,1)} %bitcast.338), calls=%async_computation.5 | async-start | bytes 4194304
  50.4 101.5 %all-to-all-start.1 = ((bf16[8,64,8192]{2,1,0:T(8,128)(2,1)}), bf16[8,64,8192]{2,1,0:T(8,128)(2,1)}, u32[]{:S(2)}, u32[]{:S(2)}) async-start(bf16[8,64,8192]{2,1,0:T(8,128)(2,1)} %stack.3), calls=%async_computation.1 | async-start | bytes 16777216 | tf_op jit(solution)/shard_map/all_to_all | solution.py:81
  58.1 252.5 %reduce-scatter.2.cloned.1.call-start = ((), (), s32[]{:S(2)}) async-start(), calls=%async_computation.4 | async-start | bytes 18874368 | tf_op jit(solution)/shard_map/reduce_scatter | solution.py:99
  151.9 61.4 %slice-start.1 = ((s8[6291456]{0:T(1024)(128)(4,1)}), s8[4194304]{0:T(1024)(128)(4,1)S(1)}, s32[]{:S(2)}) async-start(s8[6291456]{0:T(1024)(128)(4,1)} %bitcast.338), calls=%async_computation.6 | async-start | bytes 8388608
  370.3 11.8 %collective-permute-start = (bf16[64,256]{1,0:T(8,128)(2,1)S(1)}, bf16[64,256]{1,0:T(8,128)(2,1)S(1)}, u32[]{:S(2)}, u32[]{:S(2)}) collective-permute-start(bf16[64,256]{1,0:T(8,128)(2,1)S(1)} %reduce_sum.29), channel_id=1, source_target_pairs={{0,7},{1,0},{2,1},{3,2},{4,3},{5,4},{6,5},{7,6},{8,15},{9,8},{10,9... | collective-permute-start | bytes 98312 | tf_op jit(solution)/shard_map/ppermute | solution.py:68
Sparse Core Ops, SparseCore 0:
  221.6 88.9 reduce-scatter.1
